TPU v7x, 32 devices: a whole 2x2x4 slice. The times are simulated.
32 devices in a mesh: lon: 4 (over z), lat: 4 (over y, x), dest: 2 (over core).
Axes of the slice: x: 2, y: 2, z: 4, core: 2. Of those that a mesh axis runs over, the one named last changes fastest.
Arguments:
- start_visits: bfloat16 [16, 16, 256, 256], P('lon', 'lat', None, 'dest'), may hold values from -6 to 6
- tiles: bfloat16 [16, 16, 4, 256, 256], P('lon', 'lat'), may hold values from -0.1875 to 0.1875
- codes: int32 [16, 16, 4], P('lon', 'lat'), may hold values from 0 to 8, as said below
- counts: int32 [16, 16], P('lon', 'lat'), may hold values from 1 to 4
- demo_nodes: int32 [4, 4, 1024], P('lon', 'lat', 'dest'), may hold values from 0 to 4095
Outputs:
- visits: bfloat16 [16, 16, 256, 256], P('lon', 'lat', None, 'dest')
- reward_grad: float32 [16, 16, 256], P('lon', 'lat')
Inputs may be any that keep to these rules, and one draw needn't show every extreme that they name: `codes`: within one cluster the used slots name different source clusters.
All inputs are finite; a program needn't handle non-finite values.
Results may differ from a plain program's by a relative error of at most 0.0064.
Values may be sent and summed in bfloat16 or wider, within the bound.
No kernel may reach another device: no remote copies, remote signals or barrier semaphores. Data moves between devices by JAX's collectives and lax.ppermute only.
A program may use at most 64 MiB of HBM per device.

v0:
```python
import jax
import jax.numpy as jnp
from jax import lax
from jax.sharding import PartitionSpec as P

STEPS = 4


def extended(array, sides, width):
    for axis, dim in sides:
        peers, length = (lax.axis_size(axis), array.shape[dim])
        up = [(i, (i + 1) % peers) for i in range(peers)]
        down = [(j, i) for i, j in up]
        last = lax.slice_in_dim(array, length - width, length, axis=dim)
        leading = lax.slice_in_dim(array, 0, width, axis=dim)
        before = lax.ppermute(last, axis, up)
        after = lax.ppermute(leading, axis, down)
        array = jnp.concatenate([before, array, after], axis=dim)
    return array


def extend(state):
    padded = extended(state, (("lon", 0), ("lat", 1)), 1)
    band = lax.axis_index("lat")
    bands = lax.axis_size("lat")
    rowpos = jnp.arange(state.shape[1] + 2, dtype=jnp.int32)
    lower = jnp.logical_and(rowpos == 0, band == 0)
    upper = jnp.logical_and(rowpos == state.shape[1] + 1, band == bands - 1)
    keep = jnp.logical_not(jnp.logical_or(lower, upper))
    padded = jnp.where(keep[None, :, None, None], padded, jnp.zeros_like(padded))
    return padded


def propagate(state, tiles, codes, counts):
    padded = extend(state)
    columns, rows_lat = (state.shape[0], state.shape[1])
    width = rows_lat + 2
    flat = padded.reshape(((columns + 2) * width,) + padded.shape[2:])
    xcoord = jnp.arange(columns, dtype=jnp.int32)[:, None, None]
    ycoord = jnp.arange(rows_lat, dtype=jnp.int32)[None, :, None]
    index = (xcoord + codes // 3) * width + ycoord + codes % 3
    source = flat[index]
    slot_ids = jnp.arange(codes.shape[-1], dtype=jnp.int32)
    used = slot_ids[None, None, :] < counts[:, :, None]
    source = jnp.where(used[..., None, None], source, jnp.zeros_like(source))
    result = jnp.einsum("abkid,abkij->abjd", source, tiles, preferred_element_type=jnp.float32)
    return result.astype(jnp.bfloat16)


def on_device(start_visits, tiles, codes, counts, demo_nodes):
    columns, rows_lat, nodes = (start_visits.shape[0], start_visits.shape[1], start_visits.shape[2])
    region_nodes = jnp.arange(columns * rows_lat * nodes, dtype=jnp.int32)
    listed = demo_nodes.reshape((-1,))
    demo_count = jnp.sum((listed[:, None] == region_nodes[None, :]).astype(jnp.float32), axis=0)
    demo_count = demo_count.reshape((columns, rows_lat, nodes))
    scale = (lax.axis_size("dest") * start_visits.shape[3]) ** (-0.5)
    state = start_visits
    total = jnp.zeros((columns, rows_lat, nodes), jnp.float32)
    for step in range(STEPS):
        state = propagate(state, tiles, codes, counts)
        term = -jnp.sum(state.astype(jnp.float32), axis=-1)
        if step == 0:
            term = term + demo_count
        total = total + lax.psum(term, "dest")
    return (state, scale * total)


def solution(mesh):
    return jax.shard_map(
        on_device,
        mesh=mesh,
        in_specs=(
            P("lon", "lat", None, "dest"),
            P("lon", "lat", None, None, None),
            P("lon", "lat", None),
            P("lon", "lat"),
            P("lon", "lat", "dest"),
        ),
        out_specs=(P("lon", "lat", None, "dest"), P("lon", "lat", None)),
        check_vma=False,
    )
```

profile of v0, /device:TPU:0, one launch (start us, length us, event | category | flops | bytes accessed | tf_op | source)
XLA Modules:
  0.0 185.4 jit_solution(6338904322555153694)
XLA Ops:
  1.7 3.1 %collective-permute-start = (bf16[1,4,256,128]{3,2,1,0:T(8,128)(2,1)S(1)}, bf16[1,4,256,128]{3,2,1,0:T(8,128)(2,1)S(1)}, u32[]{:S(2)}, u32[]{:S(2)}) collective-permute-start(bf16[1,4,256,128]{3,2,1,0:T(8,128)(2,1)S(1)} %get-tuple-element.21), channel_id=1, source_target_pairs={{0,8},{8,16},{16,24},{24,0},{1,9},{9,17},{17,25},{25,1},{2,10},{10... | collective-permute-start | bytes 786440 | tf_op jit(solution)/shard_map/ppermute | solution.py:16
  7.6 6.4 %collective-permute-done = bf16[1,4,256,128]{3,2,1,0:T(8,128)(2,1)S(1)} collective-permute-done((bf16[1,4,256,128]{3,2,1,0:T(8,128)(2,1)S(1)}, bf16[1,4,256,128]{3,2,1,0:T(8,128)(2,1)S(1)}, u32[]{:S(2)}, u32[]{:S(2)}) %collective-permute-start) | collective-permute-done | bytes 262176 | tf_op jit(solution)/shard_map/ppermute | solution.py:16
  22.7 9.7 %collective-permute-done.2 = bf16[6,1,256,128]{3,2,1,0:T(8,128)(2,1)S(1)} collective-permute-done((bf16[6,1,256,128]{3,2,1,0:T(8,128)(2,1)S(1)}, bf16[6,1,256,128]{3,2,1,0:T(8,128)(2,1)S(1)}, u32[]{:S(2)}, u32[]{:S(2)}) %collective-permute-start.2) | collective-permute-done | bytes 393248 | tf_op jit(solution)/shard_map/ppermute | solution.py:16
  32.4 7.0 %collective-permute-done.3 = bf16[6,1,256,128]{3,2,1,0:T(8,128)(2,1)S(1)} collective-permute-done((bf16[6,1,256,128]{3,2,1,0:T(8,128)(2,1)S(1)}, bf16[6,1,256,128]{3,2,1,0:T(8,128)(2,1)S(1)}, u32[]{:S(2)}, u32[]{:S(2)}) %collective-permute-start.3) | collective-permute-done | bytes 393248 | tf_op jit(solution)/shard_map/ppermute | solution.py:17
  45.4 2.8 %gather_fusion = bf16[64,256,128]{1,2,0:T(8,128)(2,1)} fusion(bf16[36,256,128]{1,2,0:T(8,128)(2,1)S(1)} %broadcast_select_fusion, s32[1024]{0:T(1024)S(1)} %pad_clamp_fusion), kind=kCustom, calls=%fused_computation | custom fusion | bytes 8388864 | tf_op jit(solution)/shard_map/gather | solution.py:42
  48.1 6.0 %convert_reduce_fusion.4 = (f32[4,4,256]{2,1,0:T(4,128)S(1)}, bf16[4,4,256,128]{2,3,1,0:T(8,128)(2,1)S(1)}) fusion(bf16[4,4,4,256,256]{4,3,2,1,0:T(8,128)(2,1)} %param.6, bf16[4,4,4,256,128]{3,4,2,1,0:T(8,128)(2,1)} %bitcast.52, pred[4,4,4]{2,1,0:T(4,128)(4,1)S(1)} %iota_compare_fusion.1), kind=kOutput, calls=%fused_computation.33 | convolution fusion | flops 1077407744 | bytes 13647936 | tf_op jit(solution)/shard_map/abkid,abkij->abjd/dot_general | solution.py:46
  58.1 7.2 %collective-permute-done.4 = bf16[1,4,256,128]{2,3,1,0:T(8,128)(2,1)S(1)} collective-permute-done((bf16[1,4,256,128]{2,3,1,0:T(8,128)(2,1)S(1)}, bf16[1,4,256,128]{2,3,1,0:T(8,128)(2,1)S(1)}, u32[]{:S(2)}, u32[]{:S(2)}) %collective-permute-start.4) | collective-permute-done | bytes 262176 | tf_op jit(solution)/shard_map/ppermute | solution.py:16
  65.3 3.3 %collective-permute-done.5 = bf16[1,4,256,128]{2,3,1,0:T(8,128)(2,1)S(1)} collective-permute-done((bf16[1,4,256,128]{2,3,1,0:T(8,128)(2,1)S(1)}, bf16[1,4,256,128]{2,3,1,0:T(8,128)(2,1)S(1)}, u32[]{:S(2)}, u32[]{:S(2)}) %collective-permute-start.5) | collective-permute-done | bytes 262176 | tf_op jit(solution)/shard_map/ppermute | solution.py:17
  71.6 10.0 %collective-permute-done.6 = bf16[6,1,256,128]{2,3,1,0:T(8,128)(2,1)S(1)} collective-permute-done((bf16[6,1,256,128]{2,3,1,0:T(8,128)(2,1)S(1)}, bf16[6,1,256,128]{2,3,1,0:T(8,128)(2,1)S(1)}, u32[]{:S(2)}, u32[]{:S(2)}) %collective-permute-start.6) | collective-permute-done | bytes 393248 | tf_op jit(solution)/shard_map/ppermute | solution.py:16
  81.6 6.5 %collective-permute-done.7 = bf16[6,1,256,128]{2,3,1,0:T(8,128)(2,1)S(1)} collective-permute-done((bf16[6,1,256,128]{2,3,1,0:T(8,128)(2,1)S(1)}, bf16[6,1,256,128]{2,3,1,0:T(8,128)(2,1)S(1)}, u32[]{:S(2)}, u32[]{:S(2)}) %collective-permute-start.7) | collective-permute-done | bytes 393248 | tf_op jit(solution)/shard_map/ppermute | solution.py:17
  89.0 2.8 %gather_fusion.1 = bf16[64,256,128]{1,2,0:T(8,128)(2,1)} fusion(bf16[36,256,128]{1,2,0:T(8,128)(2,1)S(1)} %bitcast_select_fusion.2, s32[1024]{0:T(1024)S(1)} %pad_clamp_fusion), kind=kCustom, calls=%fused_computation.1 | custom fusion | bytes 8388864 | tf_op jit(solution)/shard_map/gather | solution.py:42
  91.7 6.0 %convert_reduce_fusion.3 = (f32[4,4,256]{2,1,0:T(4,128)S(1)}, bf16[4,4,256,128]{2,3,1,0:T(8,128)(2,1)S(1)}) fusion(bf16[4,4,4,256,256]{4,3,2,1,0:T(8,128)(2,1)} %param.6, bf16[4,4,4,256,128]{3,4,2,1,0:T(8,128)(2,1)} %bitcast.53, pred[4,4,4]{2,1,0:T(4,128)(4,1)S(1)} %iota_compare_fusion.1), kind=kOutput, calls=%fused_computation.32 | convolution fusion | flops 1077407744 | bytes 13647936 | tf_op jit(solution)/shard_map/abkid,abkij->abjd/dot_general | solution.py:46
  98.2 3.4 %collective-permute-start.9 = (bf16[1,4,256,128]{2,3,1,0:T(8,128)(2,1)S(1)}, bf16[1,4,256,128]{2,3,1,0:T(8,128)(2,1)S(1)}, u32[]{:S(2)}, u32[]{:S(2)}) collective-permute-start(bf16[1,4,256,128]{2,3,1,0:T(8,128)(2,1)S(1)} %get-tuple-element.17), channel_id=1, source_target_pairs={{8,0},{16,8},{24,16},{0,24},{9,1},{17,9},{25,17},{1,25},{10,2},{18... | collective-permute-start | bytes 786440 | tf_op jit(solution)/shard_map/ppermute | solution.py:17
  101.7 7.2 %collective-permute-done.8 = bf16[1,4,256,128]{2,3,1,0:T(8,128)(2,1)S(1)} collective-permute-done((bf16[1,4,256,128]{2,3,1,0:T(8,128)(2,1)S(1)}, bf16[1,4,256,128]{2,3,1,0:T(8,128)(2,1)S(1)}, u32[]{:S(2)}, u32[]{:S(2)}) %collective-permute-start.8) | collective-permute-done | bytes 262176 | tf_op jit(solution)/shard_map/ppermute | solution.py:16
  114.0 10.0 %collective-permute-done.10 = bf16[6,1,256,128]{2,3,1,0:T(8,128)(2,1)S(1)} collective-permute-done((bf16[6,1,256,128]{2,3,1,0:T(8,128)(2,1)S(1)}, bf16[6,1,256,128]{2,3,1,0:T(8,128)(2,1)S(1)}, u32[]{:S(2)}, u32[]{:S(2)}) %collective-permute-start.10) | collective-permute-done | bytes 393248 | tf_op jit(solution)/shard_map/ppermute | solution.py:16
  123.9 5.8 %collective-permute-done.11 = bf16[6,1,256,128]{2,3,1,0:T(8,128)(2,1)S(1)} collective-permute-done((bf16[6,1,256,128]{2,3,1,0:T(8,128)(2,1)S(1)}, bf16[6,1,256,128]{2,3,1,0:T(8,128)(2,1)S(1)}, u32[]{:S(2)}, u32[]{:S(2)}) %collective-permute-start.11) | collective-permute-done | bytes 393248 | tf_op jit(solution)/shard_map/ppermute | solution.py:17
  130.6 2.8 %gather_fusion.2 = bf16[64,256,128]{1,2,0:T(8,128)(2,1)} fusion(bf16[36,256,128]{1,2,0:T(8,128)(2,1)S(1)} %bitcast_select_fusion.1, s32[1024]{0:T(1024)S(1)} %pad_clamp_fusion), kind=kCustom, calls=%fused_computation.2 | custom fusion | bytes 8388864 | tf_op jit(solution)/shard_map/gather | solution.py:42
  133.3 6.0 %convert_reduce_fusion.2 = (f32[4,4,256]{2,1,0:T(4,128)S(1)}, bf16[4,4,256,128]{2,3,1,0:T(8,128)(2,1)S(1)}) fusion(bf16[4,4,4,256,256]{4,3,2,1,0:T(8,128)(2,1)} %param.6, bf16[4,4,4,256,128]{3,4,2,1,0:T(8,128)(2,1)} %bitcast.54, pred[4,4,4]{2,1,0:T(4,128)(4,1)S(1)} %iota_compare_fusion.1), kind=kOutput, calls=%fused_computation.31 | convolution fusion | flops 1077407744 | bytes 13647936 | tf_op jit(solution)/shard_map/abkid,abkij->abjd/dot_general | solution.py:46
  139.7 3.5 %collective-permute-start.13 = (bf16[1,4,256,128]{2,3,1,0:T(8,128)(2,1)S(1)}, bf16[1,4,256,128]{2,3,1,0:T(8,128)(2,1)S(1)}, u32[]{:S(2)}, u32[]{:S(2)}) collective-permute-start(bf16[1,4,256,128]{2,3,1,0:T(8,128)(2,1)S(1)} %get-tuple-element.15), channel_id=1, source_target_pairs={{8,0},{16,8},{24,16},{0,24},{9,1},{17,9},{25,17},{1,25},{10,2},{18... | collective-permute-start | bytes 786440 | tf_op jit(solution)/shard_map/ppermute | solution.py:17
  143.3 6.6 %collective-permute-done.12 = bf16[1,4,256,128]{2,3,1,0:T(8,128)(2,1)S(1)} collective-permute-done((bf16[1,4,256,128]{2,3,1,0:T(8,128)(2,1)S(1)}, bf16[1,4,256,128]{2,3,1,0:T(8,128)(2,1)S(1)}, u32[]{:S(2)}, u32[]{:S(2)}) %collective-permute-start.12) | collective-permute-done | bytes 262176 | tf_op jit(solution)/shard_map/ppermute | solution.py:16
  156.8 7.9 %collective-permute-done.14 = bf16[6,1,256,128]{2,3,1,0:T(8,128)(2,1)S(1)} collective-permute-done((bf16[6,1,256,128]{2,3,1,0:T(8,128)(2,1)S(1)}, bf16[6,1,256,128]{2,3,1,0:T(8,128)(2,1)S(1)}, u32[]{:S(2)}, u32[]{:S(2)}) %collective-permute-start.14) | collective-permute-done | bytes 393248 | tf_op jit(solution)/shard_map/ppermute | solution.py:16
  164.7 5.8 %collective-permute-done.15 = bf16[6,1,256,128]{2,3,1,0:T(8,128)(2,1)S(1)} collective-permute-done((bf16[6,1,256,128]{2,3,1,0:T(8,128)(2,1)S(1)}, bf16[6,1,256,128]{2,3,1,0:T(8,128)(2,1)S(1)}, u32[]{:S(2)}, u32[]{:S(2)}) %collective-permute-start.15) | collective-permute-done | bytes 393248 | tf_op jit(solution)/shard_map/ppermute | solution.py:17
  174.1 6.0 %convert_reduce_fusion.1 = (f32[4,4,256]{2,1,0:T(4,128)S(1)}, bf16[4,4,256,128]{2,3,1,0:T(8,128)(2,1)S(1)}) fusion(bf16[4,4,4,256,256]{4,3,2,1,0:T(8,128)(2,1)} %param.6, bf16[4,4,4,256,128]{3,4,2,1,0:T(8,128)(2,1)} %bitcast.51, pred[4,4,4]{2,1,0:T(4,128)(4,1)S(1)} %iota_compare_fusion.1), kind=kOutput, calls=%fused_computation.30 | convolution fusion | flops 1077407744 | bytes 13647936 | tf_op jit(solution)/shard_map/abkid,abkij->abjd/dot_general | solution.py:46
  180.1 3.4 %psum.34 = f32[4,4,256]{2,1,0:T(4,128)S(1)} all-reduce(f32[4,4,256]{2,1,0:T(4,128)S(1)} %bitcast.56), channel_id=1, replica_groups=mesh['lon'=4,'lat'=4,'dest'=2] {'dest'}, use_global_device_ids=true, to_apply=%region_2.3 | all-reduce | flops 4096 | bytes 32768 | tf_op jit(solution)/shard_map/psum | solution.py:64
  (55 shorter events, 45.7 us)
Async XLA Ops:
  1.7 12.3 %collective-permute-start = (bf16[1,4,256,128]{3,2,1,0:T(8,128)(2,1)S(1)}, bf16[1,4,256,128]{3,2,1,0:T(8,128)(2,1)S(1)}, u32[]{:S(2)}, u32[]{:S(2)}) collective-permute-start(bf16[1,4,256,128]{3,2,1,0:T(8,128)(2,1)S(1)} %get-tuple-element.21), channel_id=1, source_target_pairs={{0,8},{8,16},{16,24},{24,0},{1,9},{9,17},{17,25},{25,1},{2,10},{10... | collective-permute-start | bytes 786440 | tf_op jit(solution)/shard_map/ppermute | solution.py:16
  4.8 13.4 %collective-permute-start.1 = (bf16[1,4,256,128]{3,2,1,0:T(8,128)(2,1)S(1)}, bf16[1,4,256,128]{3,2,1,0:T(8,128)(2,1)S(1)}, u32[]{:S(2)}, u32[]{:S(2)}) collective-permute-start(bf16[1,4,256,128]{3,2,1,0:T(8,128)(2,1)S(1)} %get-tuple-element.20), channel_id=1, source_target_pairs={{8,0},{16,8},{24,16},{0,24},{9,1},{17,9},{25,17},{1,25},{10,2},{18... | collective-permute-start | bytes 786440 | tf_op jit(solution)/shard_map/ppermute | solution.py:17
  7.6 15.0 %copy-start.1 = (s32[4,4]{1,0:T(4,128)S(1)}, s32[4,4]{1,0:T(4,128)}, u32[]{:S(2)}) copy-start(s32[4,4]{1,0:T(4,128)} %param.8) | copy-start | bytes 196
  18.2 1.2 copy-start
  19.4 12.9 %collective-permute-start.2 = (bf16[6,1,256,128]{3,2,1,0:T(8,128)(2,1)S(1)}, bf16[6,1,256,128]{3,2,1,0:T(8,128)(2,1)S(1)}, u32[]{:S(2)}, u32[]{:S(2)}) collective-permute-start(bf16[6,1,256,128]{3,2,1,0:T(8,128)(2,1)S(1)} %get-tuple-element.12), channel_id=1, source_target_pairs={{0,2},{2,4},{4,6},{6,0},{1,3},{3,5},{5,7},{7,1},{8,10},{10,12},{12... | collective-permute-start | bytes 1179656 | tf_op jit(solution)/shard_map/ppermute | solution.py:16
  21.0 18.4 %collective-permute-start.3 = (bf16[6,1,256,128]{3,2,1,0:T(8,128)(2,1)S(1)}, bf16[6,1,256,128]{3,2,1,0:T(8,128)(2,1)S(1)}, u32[]{:S(2)}, u32[]{:S(2)}) collective-permute-start(bf16[6,1,256,128]{3,2,1,0:T(8,128)(2,1)S(1)} %get-tuple-element.13), channel_id=1, source_target_pairs={{2,0},{4,2},{6,4},{0,6},{3,1},{5,3},{7,5},{1,7},{10,8},{12,10},{14... | collective-permute-start | bytes 1179656 | tf_op jit(solution)/shard_map/ppermute | solution.py:17
  54.2 11.1 %collective-permute-start.4 = (bf16[1,4,256,128]{2,3,1,0:T(8,128)(2,1)S(1)}, bf16[1,4,256,128]{2,3,1,0:T(8,128)(2,1)S(1)}, u32[]{:S(2)}, u32[]{:S(2)}) collective-permute-start(bf16[1,4,256,128]{2,3,1,0:T(8,128)(2,1)S(1)} %get-tuple-element.18), channel_id=1, source_target_pairs={{0,8},{8,16},{16,24},{24,0},{1,9},{9,17},{17,25},{25,1},{2,10},{10... | collective-permute-start | bytes 786440 | tf_op jit(solution)/shard_map/ppermute | solution.py:16
  55.9 12.6 %collective-permute-start.5 = (bf16[1,4,256,128]{2,3,1,0:T(8,128)(2,1)S(1)}, bf16[1,4,256,128]{2,3,1,0:T(8,128)(2,1)S(1)}, u32[]{:S(2)}, u32[]{:S(2)}) collective-permute-start(bf16[1,4,256,128]{2,3,1,0:T(8,128)(2,1)S(1)} %get-tuple-element.19), channel_id=1, source_target_pairs={{8,0},{16,8},{24,16},{0,24},{9,1},{17,9},{25,17},{1,25},{10,2},{18... | collective-permute-start | bytes 786440 | tf_op jit(solution)/shard_map/ppermute | solution.py:17
  68.7 12.9 %collective-permute-start.6 = (bf16[6,1,256,128]{2,3,1,0:T(8,128)(2,1)S(1)}, bf16[6,1,256,128]{2,3,1,0:T(8,128)(2,1)S(1)}, u32[]{:S(2)}, u32[]{:S(2)}) collective-permute-start(bf16[6,1,256,128]{2,3,1,0:T(8,128)(2,1)S(1)} %get-tuple-element.10), channel_id=1, source_target_pairs={{0,2},{2,4},{4,6},{6,0},{1,3},{3,5},{5,7},{7,1},{8,10},{10,12},{12... | collective-permute-start | bytes 1179656 | tf_op jit(solution)/shard_map/ppermute | solution.py:16
  70.2 17.9 %collective-permute-start.7 = (bf16[6,1,256,128]{2,3,1,0:T(8,128)(2,1)S(1)}, bf16[6,1,256,128]{2,3,1,0:T(8,128)(2,1)S(1)}, u32[]{:S(2)}, u32[]{:S(2)}) collective-permute-start(bf16[6,1,256,128]{2,3,1,0:T(8,128)(2,1)S(1)} %get-tuple-element.11), channel_id=1, source_target_pairs={{2,0},{4,2},{6,4},{0,6},{3,1},{5,3},{7,5},{1,7},{10,8},{12,10},{14... | collective-permute-start | bytes 1179656 | tf_op jit(solution)/shard_map/ppermute | solution.py:17
  97.8 11.0 %collective-permute-start.8 = (bf16[1,4,256,128]{2,3,1,0:T(8,128)(2,1)S(1)}, bf16[1,4,256,128]{2,3,1,0:T(8,128)(2,1)S(1)}, u32[]{:S(2)}, u32[]{:S(2)}) collective-permute-start(bf16[1,4,256,128]{2,3,1,0:T(8,128)(2,1)S(1)} %get-tuple-element.16), channel_id=1, source_target_pairs={{0,8},{8,16},{16,24},{24,0},{1,9},{9,17},{17,25},{25,1},{2,10},{10... | collective-permute-start | bytes 786440 | tf_op jit(solution)/shard_map/ppermute | solution.py:16
  98.2 12.7 %collective-permute-start.9 = (bf16[1,4,256,128]{2,3,1,0:T(8,128)(2,1)S(1)}, bf16[1,4,256,128]{2,3,1,0:T(8,128)(2,1)S(1)}, u32[]{:S(2)}, u32[]{:S(2)}) collective-permute-start(bf16[1,4,256,128]{2,3,1,0:T(8,128)(2,1)S(1)} %get-tuple-element.17), channel_id=1, source_target_pairs={{8,0},{16,8},{24,16},{0,24},{9,1},{17,9},{25,17},{1,25},{10,2},{18... | collective-permute-start | bytes 786440 | tf_op jit(solution)/shard_map/ppermute | solution.py:17
  111.0 12.9 %collective-permute-start.10 = (bf16[6,1,256,128]{2,3,1,0:T(8,128)(2,1)S(1)}, bf16[6,1,256,128]{2,3,1,0:T(8,128)(2,1)S(1)}, u32[]{:S(2)}, u32[]{:S(2)}) collective-permute-start(bf16[6,1,256,128]{2,3,1,0:T(8,128)(2,1)S(1)} %get-tuple-element.8), channel_id=1, source_target_pairs={{0,2},{2,4},{4,6},{6,0},{1,3},{3,5},{5,7},{7,1},{8,10},{10,12},{12... | collective-permute-start | bytes 1179656 | tf_op jit(solution)/shard_map/ppermute | solution.py:16
  112.5 17.2 %collective-permute-start.11 = (bf16[6,1,256,128]{2,3,1,0:T(8,128)(2,1)S(1)}, bf16[6,1,256,128]{2,3,1,0:T(8,128)(2,1)S(1)}, u32[]{:S(2)}, u32[]{:S(2)}) collective-permute-start(bf16[6,1,256,128]{2,3,1,0:T(8,128)(2,1)S(1)} %get-tuple-element.9), channel_id=1, source_target_pairs={{2,0},{4,2},{6,4},{0,6},{3,1},{5,3},{7,5},{1,7},{10,8},{12,10},{14... | collective-permute-start | bytes 1179656 | tf_op jit(solution)/shard_map/ppermute | solution.py:17
  139.3 15.5 %copy-start.2 = (s32[1,1,512]{2,1,0:T(1,128)S(1)}, s32[1,1,512]{2,1,0:T(1,128)}, u32[]{:S(2)}) copy-start(s32[1,1,512]{2,1,0:T(1,128)} %param.9) | copy-start | bytes 6148
  139.4 10.4 %collective-permute-start.12 = (bf16[1,4,256,128]{2,3,1,0:T(8,128)(2,1)S(1)}, bf16[1,4,256,128]{2,3,1,0:T(8,128)(2,1)S(1)}, u32[]{:S(2)}, u32[]{:S(2)}) collective-permute-start(bf16[1,4,256,128]{2,3,1,0:T(8,128)(2,1)S(1)} %get-tuple-element.14), channel_id=1, source_target_pairs={{0,8},{8,16},{16,24},{24,0},{1,9},{9,17},{17,25},{25,1},{2,10},{10... | collective-permute-start | bytes 786440 | tf_op jit(solution)/shard_map/ppermute | solution.py:16
  139.7 12.0 %collective-permute-start.13 = (bf16[1,4,256,128]{2,3,1,0:T(8,128)(2,1)S(1)}, bf16[1,4,256,128]{2,3,1,0:T(8,128)(2,1)S(1)}, u32[]{:S(2)}, u32[]{:S(2)}) collective-permute-start(bf16[1,4,256,128]{2,3,1,0:T(8,128)(2,1)S(1)} %get-tuple-element.15), channel_id=1, source_target_pairs={{8,0},{16,8},{24,16},{0,24},{9,1},{17,9},{25,17},{1,25},{10,2},{18... | collective-permute-start | bytes 786440 | tf_op jit(solution)/shard_map/ppermute | solution.py:17
  151.8 12.9 %collective-permute-start.14 = (bf16[6,1,256,128]{2,3,1,0:T(8,128)(2,1)S(1)}, bf16[6,1,256,128]{2,3,1,0:T(8,128)(2,1)S(1)}, u32[]{:S(2)}, u32[]{:S(2)}) collective-permute-start(bf16[6,1,256,128]{2,3,1,0:T(8,128)(2,1)S(1)} %get-tuple-element.6), channel_id=1, source_target_pairs={{0,2},{2,4},{4,6},{6,0},{1,3},{3,5},{5,7},{7,1},{8,10},{10,12},{12... | collective-permute-start | bytes 1179656 | tf_op jit(solution)/shard_map/ppermute | solution.py:16
  153.4 17.2 %collective-permute-start.15 = (bf16[6,1,256,128]{2,3,1,0:T(8,128)(2,1)S(1)}, bf16[6,1,256,128]{2,3,1,0:T(8,128)(2,1)S(1)}, u32[]{:S(2)}, u32[]{:S(2)}) collective-permute-start(bf16[6,1,256,128]{2,3,1,0:T(8,128)(2,1)S(1)} %get-tuple-element.7), channel_id=1, source_target_pairs={{2,0},{4,2},{6,4},{0,6},{3,1},{5,3},{7,5},{1,7},{10,8},{12,10},{14... | collective-permute-start | bytes 1179656 | tf_op jit(solution)/shard_map/ppermute | solution.py:17
where the time goes:
time: 186 us; the launch traced here: 185 us
  waiting for transfers between devices  99.9 us (54%)
  starting transfers between devices  28.7 us (15%)
  matrix products  23.9 us (13%)
  local copies, waits for them, and re-layouts  18.8 us (10%)
  other arithmetic  9.83 us (5%)
  blocking collectives  3.36 us (2%)
    ppermute x8, waiting for transfers between devices, extended(): before = lax.ppermute(last, axis, up)  64.8 us
    ppermute x8, waiting for transfers between devices, extended(): after = lax.ppermute(leading, axis, down)  35.1 us
    dot_general x4, matrix products, propagate(): jnp.einsum('abkid,abkij->abjd', source, tiles, preferred_element_type=jnp...  23.9 us
    ppermute x8, starting transfers between devices, extended(): after = lax.ppermute(leading, axis, down)  17 us
    ppermute x8, starting transfers between devices, extended(): before = lax.ppermute(last, axis, up)  11.8 us
    gather x4, local copies, waits for them, and re-layouts, propagate(): source = flat[index]  11 us
    unnamed x9, local copies, waits for them, and re-layouts  3.88 us
  transfers between devices with their start and end apart: 16, of which 16 were waited for; matrix products, arithmetic and copies ran while one was open for 2% of the time, Pallas kernels for 0%

commit v1 on v0

v1 whole, which is shorter than its diff:
```python
import functools

import jax
import jax.numpy as jnp
from jax import lax
from jax.experimental import pallas as pl
from jax.experimental.pallas import tpu as pltpu
from jax.sharding import PartitionSpec as P


STEPS = 4
VMEM = pltpu.VMEM
ANY = pl.ANY
LIMIT = 24 * 1024 * 1024


def pairs(peers):
    if peers % 2 == 0:
        first = [(i, i ^ 1) for i in range(peers)]
        second = [(i, (i + 1) % peers if i % 2 else (i - 1) % peers) for i in range(peers)]
        return first, second
    up = [(i, (i + 1) % peers) for i in range(peers)]
    return up, [(j, i) for i, j in up]


def sides(axis):
    peers, me = lax.axis_size(axis), lax.axis_index(axis)
    if peers % 2 == 0:
        return me % 2, me % 2
    return jnp.int32(0), jnp.int32(1)


def swap(messages, axis):
    received = []
    for message, moves in zip(messages, pairs(lax.axis_size(axis))):
        received.append(lax.ppermute(message, axis, moves))
    return received


def call(kernel, outs, args, flops=0, scratch=(), same=None, plain=()):
    same = same or {}
    loose = {i for i, o in same.items() if o in plain}
    args = [a if i in loose else pltpu.with_memory_space_constraint(a, VMEM) for i, a in enumerate(args)]
    spec = lambda free: pl.BlockSpec(memory_space=ANY if free else VMEM)
    return pl.pallas_call(
        kernel,
        out_shape=[jax.ShapeDtypeStruct(*o) if i in plain else VMEM(*o) for i, o in enumerate(outs)],
        in_specs=[spec(i in loose) for i in range(len(args))],
        out_specs=[spec(i in plain) for i in range(len(outs))],
        scratch_shapes=list(scratch),
        input_output_aliases=same,
        compiler_params=pltpu.CompilerParams(vmem_limit_bytes=LIMIT),
        cost_estimate=pl.CostEstimate(flops=flops, bytes_accessed=1 << 20, transcendentals=0),
    )(*args)


def hold_kernel(source, held, sem):
    copy = pltpu.make_async_copy(source, held, sem)
    copy.start()
    copy.wait()


def hold(array):
    return pl.pallas_call(
        hold_kernel,
        name="hold",
        out_shape=VMEM(array.shape, array.dtype),
        in_specs=[pl.BlockSpec(memory_space=ANY)],
        out_specs=pl.BlockSpec(memory_space=VMEM),
        scratch_shapes=[pltpu.SemaphoreType.DMA],
        compiler_params=pltpu.CompilerParams(vmem_limit_bytes=LIMIT),
        cost_estimate=pl.CostEstimate(flops=1 << 22, bytes_accessed=array.size * 2, transcendentals=0),
    )(pltpu.with_memory_space_constraint(array, pltpu.HBM))


def put_edges(shape, state, messages):
    columns, rows = shape
    lon, lat = sides("lon")[0], sides("lat")[0]
    for m in (0, 1):
        x = jnp.where(lon == m, columns - 1, 0)
        for y in range(rows):
            messages[m][y] = state[x * rows + y]
        y = jnp.where(lat == m, rows - 1, 0)
        for x in range(columns):
            messages[2 + m][x] = state[x * rows + y]


def prep_kernel(shape, start, state, *messages):
    for c in range(shape[0] * shape[1]):
        state[c] = start[c].T
    put_edges(shape, state, messages)


def corner_kernel(rows, r0, r1, q0, q1):
    low_first = sides("lon")[1] == 1
    upward = sides("lat")[0]
    for m, ref in enumerate((q0, q1)):
        y = jnp.where(upward == m, rows - 1, 0)
        ref[0] = jnp.where(low_first, r0[y], r1[y])
        ref[1] = jnp.where(low_first, r1[y], r0[y])


def corner_places(shape):
    columns, rows = shape
    ends = {x * rows + y for x in (0, columns - 1) for y in (0, rows - 1)}
    return sorted(ends)


def cluster(c, slots, idx, pool, tiles):
    entries = [divmod(c * slots + k, 128) for k in range(slots)]
    picks = [idx[i : i + 1, :][0, j] for i, j in entries]
    lhs = jnp.concatenate([pool[p] for p in picks], axis=1)
    value = jnp.dot(lhs, tiles[c], preferred_element_type=jnp.float32).astype(jnp.bfloat16)
    share, nodes = value.shape
    return value, value.astype(jnp.float32).reshape(share // 8, 8, nodes).sum(axis=0)


def emit(places, shape, slots, idx, pool, tiles, tot, results, last):
    if last:
        demo, out, grad, turned, sems = results
        for c in places:
            value, sums = cluster(c, slots, idx, pool, tiles)
            turned[c] = value.T
            pltpu.make_async_copy(turned.at[c], out.at[c], sems.at[c]).start()
            x, y = divmod(c, shape[1])
            parts = value.shape[1] // demo.shape[1]
            seen = jnp.concatenate([demo[i : i + 1, :] for i in range(c * parts, (c + 1) * parts)], axis=1)
            grad[x, y : y + 1, :] = seen - (tot[c] + sums).sum(axis=0, keepdims=True)
        for c in places:
            pltpu.make_async_copy(turned.at[c], out.at[c], sems.at[c]).wait()
    else:
        new, tot_out = results
        for c in places:
            value, sums = cluster(c, slots, idx, pool, tiles)
            new[c] = value
            tot_out[c] = tot[c] + sums


def main_kernel(shape, slots, last, *refs):
    idx, state, *halo, tiles, tot = refs[:8]
    clusters = shape[0] * shape[1]
    if last:
        demo, out, grad, pool, turned, sems = refs[8:]
        results = demo, out, grad, turned, sems
    else:
        new, tot_out, pool = refs[8:]
        results = new, tot_out
    at = 0
    for part in (state, *halo):
        for i in range(part.shape[0]):
            pool[at + i] = part[i]
        at += part.shape[0]
    pool[at] = jnp.zeros(pool.shape[1:], pool.dtype)
    corners = corner_places(shape)
    emit([c for c in range(clusters) if c not in corners], shape, slots, idx, pool, tiles, tot, results, last)


def tail_kernel(shape, slots, last, *refs):
    idx, q0, q1, tiles, tot, _, _, _ = refs[:8]
    if last:
        demo, out, grad, pool, turned, sems = refs[8:]
        results = demo, out, grad, turned, sems
    else:
        new, tot_out, pool, *messages = refs[8:]
        results = new, tot_out
    at = pool.shape[0] - 4
    for i, (part, j) in enumerate(((q0, 0), (q0, 1), (q1, 0), (q1, 1))):
        pool[at + i] = part[j]
    emit(corner_places(shape), shape, slots, idx, pool, tiles, tot, results, last)
    if not last:
        put_edges(shape, new, messages)


def demo_kernel(nodes_ref, counts_ref):
    listed = nodes_ref[...]
    high, low = counts_ref.shape
    entries = listed.shape[1]
    up = lax.broadcasted_iota(jnp.int32, (high, entries), 0) == listed // low
    down = lax.broadcasted_iota(jnp.int32, (low, entries), 0) == listed % low
    counts_ref[...] = lax.dot_general(
        up.astype(jnp.bfloat16),
        down.astype(jnp.bfloat16),
        (((1,), (1,)), ((), ())),
        preferred_element_type=jnp.float32,
    )


def sources(codes, counts, shape):
    columns, rows = shape
    clusters = columns * rows
    slots = codes.shape[-1]
    hi_lon, hi_lat = sides("lon")[1], sides("lat")[1]
    xcoord = jnp.arange(columns, dtype=jnp.int32)[:, None, None]
    ycoord = jnp.arange(rows, dtype=jnp.int32)[None, :, None]
    sx, sy = xcoord + codes // 3 - 1, ycoord + codes % 3 - 1
    inx = jnp.logical_and(sx >= 0, sx < columns)
    iny = jnp.logical_and(sy >= 0, sy < rows)
    by_lon = jnp.where(sx < 0, 1 - hi_lon, hi_lon)
    by_lat = jnp.where(sy < 0, 1 - hi_lat, hi_lat)
    band, bands = lax.axis_index("lat"), lax.axis_size("lat")
    outside = jnp.logical_or(
        jnp.logical_and(band == 0, sy < 0), jnp.logical_and(band == bands - 1, sy >= rows)
    )
    unused = jnp.arange(slots, dtype=jnp.int32)[None, None, :] >= counts[:, :, None]
    second = clusters + 2 * rows
    zero = second + 2 * columns
    source = jnp.where(
        iny,
        jnp.where(inx, sx * rows + sy, clusters + by_lon * rows + sy),
        jnp.where(inx, second + by_lat * columns + sx, zero + 1 + by_lat * 2 + (sx >= columns)),
    )
    source = jnp.where(jnp.logical_or(outside, unused), zero, source).reshape(-1)
    return jnp.pad(source, (0, -source.size % 128)).reshape(-1, 128), zero + 5


def on_device(start_visits, tiles, codes, counts, demo_nodes):
    columns, rows, nodes, dests = start_visits.shape
    slots = codes.shape[-1]
    clusters = columns * rows
    shape = (columns, rows)
    scale = (lax.axis_size("dest") * dests) ** (-0.5)
    idx, depth = sources(codes, counts, shape)

    bf, f32 = jnp.bfloat16, jnp.float32
    block = lambda n: ((n, dests, nodes), bf)
    low = min(nodes, 128)
    (demo,) = call(demo_kernel, [((clusters * nodes // low, low), f32)], [demo_nodes.reshape(1, -1)])
    weights = hold(tiles.reshape(clusters, slots * nodes, nodes))
    tot = jnp.zeros((clusters, 8, nodes), f32)
    sums = (tot.shape, f32)
    edges = [block(rows)] * 2 + [block(columns)] * 2
    state, *messages = call(
        functools.partial(prep_kernel, shape), [block(clusters), *edges], [start_visits.reshape(clusters, nodes, dests)]
    )
    work = 2 * clusters * slots * nodes * nodes * dests
    for step in range(STEPS):
        last = step == STEPS - 1
        lon = swap(messages[:2], "lon")
        lat = swap(messages[2:], "lat")
        ends = call(functools.partial(corner_kernel, rows), [block(2)] * 2, lon)
        ends = swap(ends, "lat")
        main = functools.partial(main_kernel, shape, slots, last)
        tail = functools.partial(tail_kernel, shape, slots, last)
        given = [idx, state, *lon, *lat, weights, tot]
        if last:
            outs = [((clusters, nodes, dests), bf), ((columns, rows, nodes), f32), block(depth)]
            scratch = [VMEM((clusters, nodes, dests), bf), pltpu.SemaphoreType.DMA((clusters,))]
            visits, grad, pool = call(main, outs, [*given, demo], work * 3 // 4, scratch, plain=(0,))
            visits, grad, _ = call(
                tail,
                outs,
                [idx, *ends, weights, tot, visits, grad, pool, demo],
                work // 4,
                scratch,
                same={5: 0, 6: 1, 7: 2},
                plain=(0,),
            )
        else:
            outs = [block(clusters), sums, block(depth)]
            new, tot_new, pool = call(main, outs, given, work * 3 // 4)
            state, tot, _, *messages = call(
                tail, outs + edges, [idx, *ends, weights, tot, new, tot_new, pool], work // 4, same={5: 0, 6: 1, 7: 2}
            )
    grad = scale * grad
    if lax.axis_size("dest") == 2:
        grad = grad + lax.ppermute(grad, "dest", [(0, 1), (1, 0)])
    else:
        grad = lax.psum(grad, "dest")
    return visits.reshape(start_visits.shape), grad


def solution(mesh):
    return jax.shard_map(
        on_device,
        mesh=mesh,
        in_specs=(
            P("lon", "lat", None, "dest"),
            P("lon", "lat", None, None, None),
            P("lon", "lat", None),
            P("lon", "lat"),
            P("lon", "lat", "dest"),
        ),
        out_specs=(P("lon", "lat", None, "dest"), P("lon", "lat", None)),
        check_vma=False,
    )
```

time: 186 us -> 93.7 us (0.50)
  waiting for transfers between devices: 99.9 us -> 39.9 us
  matrix products: 23.9 us -> 0 us
  local copies, waits for them, and re-layouts: 18.8 us -> 1.33 us
  Pallas kernels: 0 us -> 13 us
  other arithmetic: 9.83 us -> 1.39 us
  starting transfers between devices: 28.7 us -> 37 us
  blocking collectives: 3.36 us -> 0 us
    ppermute x16 -> x25, waiting for transfers between devices: 99.9 us -> 39.9 us  [the longest x24 38.8 us: swap(): received.append(lax.ppermute(message, axis, moves))]
    dot_general x4 -> x0, matrix products: 23.9 us -> none  [propagate(): jnp.einsum('abkid,abkij->abjd', source, tiles, preferred_element_type=jnp...]
    pallas_call x0 -> x15, Pallas kernels: none -> 13 us  [the longest x14 9.62 us: call(): pl.pallas_call(kernel, out_shape=[jax.ShapeDtypeStruct(*o) if i in plain...]
    gather x4 -> x0, local copies, waits for them, and re-layouts: 11 us -> none  [propagate(): source = flat[index]]
    ppermute x16 -> x25, starting transfers between devices: 28.7 us -> 37 us  [the longest x24 37 us: swap(): received.append(lax.ppermute(message, axis, moves))]
    psum x1 -> x0, blocking collectives: 3.36 us -> none  [on_device(): total = total + lax.psum(term, 'dest')]
    select_n x5 -> x1, other arithmetic: 3.95 us -> 0.77 us  [sources(): jnp.where(jnp.logical_or(outside, unused), zero, source).reshape(-1)]
    concatenate x4 -> x0, other arithmetic: 2.89 us -> none  [extended(): array = jnp.concatenate([before, array, after], axis=dim)]
  transfers between devices with their start and end apart: 16 -> 25, of which waited for: 16 -> 16; matrix products, arithmetic and copies ran while one was open for 2% -> 1% of each run, Pallas kernels for 0% -> 10%
where the time goes in v1:
time: 93.7 us; the launch traced here: 93.5 us
  waiting for transfers between devices  39.9 us (43%)
  starting transfers between devices  37 us (39%)
  Pallas kernels  13 us (14%)
  other arithmetic  1.39 us (1%)
  local copies, waits for them, and re-layouts  1.33 us (1%)
    ppermute x24, waiting for transfers between devices, swap(): received.append(lax.ppermute(message, axis, moves))  38.8 us
    ppermute x24, starting transfers between devices, swap(): received.append(lax.ppermute(message, axis, moves))  37 us
    pallas_call x14, Pallas kernels, call(): pl.pallas_call(kernel, out_shape=[jax.ShapeDtypeStruct(*o) if i in plain...  9.62 us
    pallas_call x1, Pallas kernels, hold(): pl.pallas_call(hold_kernel, name='hold', out_shape=VMEM(array.shape, arra...  3.39 us
  transfers between devices with their start and end apart: 25, of which 16 were waited for; matrix products, arithmetic and copies ran while one was open for 1% of the time, Pallas kernels for 10%

profile of v1, /device:TPU:0, one launch (start us, length us, event | category | flops | bytes accessed | tf_op | source)
XLA Modules:
  0.0 93.5 jit_solution(1299221828839594238)
XLA Ops:
  2.3 3.1 %collective-permute-start = (bf16[4,128,256]{2,1,0:T(8,128)(2,1)S(1)}, bf16[4,128,256]{2,1,0:T(8,128)(2,1)S(1)}, u32[]{:S(2)}, u32[]{:S(2)}) collective-permute-start(bf16[4,128,256]{2,1,0:T(8,128)(2,1)S(1)} %get-tuple-element.47), channel_id=1, source_target_pairs={{0,8},{8,0},{16,24},{24,16},{1,9},{9,1},{17,25},{25,17},{2,10},{10... | collective-permute-start | bytes 786440 | tf_op jit(solution)/shard_map/ppermute | solution.py:36
  5.4 2.5 %collective-permute-start.1 = (bf16[4,128,256]{2,1,0:T(8,128)(2,1)S(1)}, bf16[4,128,256]{2,1,0:T(8,128)(2,1)S(1)}, u32[]{:S(2)}, u32[]{:S(2)}) collective-permute-start(bf16[4,128,256]{2,1,0:T(8,128)(2,1)S(1)} %get-tuple-element.48), channel_id=1, source_target_pairs={{0,24},{8,16},{16,8},{24,0},{1,25},{9,17},{17,9},{25,1},{2,26},{10... | collective-permute-start | bytes 786440 | tf_op jit(solution)/shard_map/ppermute | solution.py:36
  7.9 1.5 %collective-permute-start.4 = (bf16[4,128,256]{2,1,0:T(8,128)(2,1)S(1)}, bf16[4,128,256]{2,1,0:T(8,128)(2,1)S(1)}, u32[]{:S(2)}, u32[]{:S(2)}) collective-permute-start(bf16[4,128,256]{2,1,0:T(8,128)(2,1)S(1)} %get-tuple-element.52), channel_id=1, source_target_pairs={{0,2},{2,0},{4,6},{6,4},{1,3},{3,1},{5,7},{7,5},{8,10},{10,8},{12,... | collective-permute-start | bytes 786440 | tf_op jit(solution)/shard_map/ppermute | solution.py:36
  9.3 1.5 %collective-permute-start.5 = (bf16[4,128,256]{2,1,0:T(8,128)(2,1)S(1)}, bf16[4,128,256]{2,1,0:T(8,128)(2,1)S(1)}, u32[]{:S(2)}, u32[]{:S(2)}) collective-permute-start(bf16[4,128,256]{2,1,0:T(8,128)(2,1)S(1)} %get-tuple-element.53), channel_id=1, source_target_pairs={{0,6},{2,4},{4,2},{6,0},{1,7},{3,5},{5,3},{7,1},{8,14},{10,12},{12... | collective-permute-start | bytes 786440 | tf_op jit(solution)/shard_map/ppermute | solution.py:36
  12.1 7.5 %collective-permute-done.1.r1.refs_3_ = bf16[4,128,256]{2,1,0:T(8,128)(2,1)S(1)} collective-permute-done((bf16[4,128,256]{2,1,0:T(8,128)(2,1)S(1)}, bf16[4,128,256]{2,1,0:T(8,128)(2,1)S(1)}, u32[]{:S(2)}, u32[]{:S(2)}) %collective-permute-start.1) | collective-permute-done | bytes 262176 | tf_op jit(solution)/shard_map/ppermute | solution.py:36
  19.6 1.6 %collective-permute-start.2 = (bf16[2,128,256]{2,1,0:T(8,128)(2,1)S(1)}, bf16[2,128,256]{2,1,0:T(8,128)(2,1)S(1)}, u32[]{:S(2)}, u32[]{:S(2)}) collective-permute-start(bf16[2,128,256]{2,1,0:T(8,128)(2,1)S(1)} %get-tuple-element.49), channel_id=1, source_target_pairs={{0,2},{2,0},{4,6},{6,4},{1,3},{3,1},{5,7},{7,5},{8,10},{10,8},{12,... | collective-permute-start | bytes 393224 | tf_op jit(solution)/shard_map/ppermute | solution.py:36
  21.2 1.5 %collective-permute-start.3 = (bf16[2,128,256]{2,1,0:T(8,128)(2,1)S(1)}, bf16[2,128,256]{2,1,0:T(8,128)(2,1)S(1)}, u32[]{:S(2)}, u32[]{:S(2)}) collective-permute-start(bf16[2,128,256]{2,1,0:T(8,128)(2,1)S(1)} %get-tuple-element.50), channel_id=1, source_target_pairs={{0,6},{2,4},{4,2},{6,0},{1,7},{3,5},{5,3},{7,1},{8,14},{10,12},{12... | collective-permute-start | bytes 393224 | tf_op jit(solution)/shard_map/ppermute | solution.py:36
  22.7 3.4 %hold.1.refs_6_.refs_3_ = bf16[16,1024,256]{2,1,0:T(8,128)(2,1)S(1)} custom-call(bf16[16,1024,256]{2,1,0:T(8,128)(2,1)} %bitcast.8), custom_call_target="tpu_custom_call" | custom-call | flops 4194304 | bytes 8388608 | tf_op jit(solution)/shard_map/hold/pallas_call | solution.py:64
  28.9 2.4 %collective-permute-start.7 = (bf16[4,128,256]{2,1,0:T(8,128)(2,1)S(1)}, bf16[4,128,256]{2,1,0:T(8,128)(2,1)S(1)}, u32[]{:S(2)}, u32[]{:S(2)}) collective-permute-start(bf16[4,128,256]{2,1,0:T(8,128)(2,1)S(1)} %get-tuple-element.58), channel_id=1, source_target_pairs={{0,24},{8,16},{16,8},{24,0},{1,25},{9,17},{17,9},{25,1},{2,26},{10... | collective-permute-start | bytes 786440 | tf_op jit(solution)/shard_map/ppermute | solution.py:36
  31.3 1.5 %collective-permute-start.10 = (bf16[4,128,256]{2,1,0:T(8,128)(2,1)S(1)}, bf16[4,128,256]{2,1,0:T(8,128)(2,1)S(1)}, u32[]{:S(2)}, u32[]{:S(2)}) collective-permute-start(bf16[4,128,256]{2,1,0:T(8,128)(2,1)S(1)} %get-tuple-element.63), channel_id=1, source_target_pairs={{0,2},{2,0},{4,6},{6,4},{1,3},{3,1},{5,7},{7,5},{8,10},{10,8},{12,... | collective-permute-start | bytes 786440 | tf_op jit(solution)/shard_map/ppermute | solution.py:36
  33.9 6.3 %collective-permute-done.6.r0.refs_2_ = bf16[4,128,256]{2,1,0:T(8,128)(2,1)S(1)} collective-permute-done((bf16[4,128,256]{2,1,0:T(8,128)(2,1)S(1)}, bf16[4,128,256]{2,1,0:T(8,128)(2,1)S(1)}, u32[]{:S(2)}, u32[]{:S(2)}) %collective-permute-start.6) | collective-permute-done | bytes 262176 | tf_op jit(solution)/shard_map/ppermute | solution.py:36
  40.3 1.6 %collective-permute-start.8 = (bf16[2,128,256]{2,1,0:T(8,128)(2,1)S(1)}, bf16[2,128,256]{2,1,0:T(8,128)(2,1)S(1)}, u32[]{:S(2)}, u32[]{:S(2)}) collective-permute-start(bf16[2,128,256]{2,1,0:T(8,128)(2,1)S(1)} %get-tuple-element.59), channel_id=1, source_target_pairs={{0,2},{2,0},{4,6},{6,4},{1,3},{3,1},{5,7},{7,5},{8,10},{10,8},{12,... | collective-permute-start | bytes 393224 | tf_op jit(solution)/shard_map/ppermute | solution.py:36
  41.8 2.0 %collective-permute-start.9 = (bf16[2,128,256]{2,1,0:T(8,128)(2,1)S(1)}, bf16[2,128,256]{2,1,0:T(8,128)(2,1)S(1)}, u32[]{:S(2)}, u32[]{:S(2)}) collective-permute-start(bf16[2,128,256]{2,1,0:T(8,128)(2,1)S(1)} %get-tuple-element.60), channel_id=1, source_target_pairs={{0,6},{2,4},{4,2},{6,0},{1,7},{3,5},{5,3},{7,1},{8,14},{10,12},{12... | collective-permute-start | bytes 393224 | tf_op jit(solution)/shard_map/ppermute | solution.py:36
  46.0 2.2 %collective-permute-done.9.refs_2_ = bf16[2,128,256]{2,1,0:T(8,128)(2,1)S(1)} collective-permute-done((bf16[2,128,256]{2,1,0:T(8,128)(2,1)S(1)}, bf16[2,128,256]{2,1,0:T(8,128)(2,1)S(1)}, u32[]{:S(2)}, u32[]{:S(2)}) %collective-permute-start.9) | collective-permute-done | bytes 131104 | tf_op jit(solution)/shard_map/ppermute | solution.py:36
  48.8 2.5 %collective-permute-start.12 = (bf16[4,128,256]{2,1,0:T(8,128)(2,1)S(1)}, bf16[4,128,256]{2,1,0:T(8,128)(2,1)S(1)}, u32[]{:S(2)}, u32[]{:S(2)}) collective-permute-start(bf16[4,128,256]{2,1,0:T(8,128)(2,1)S(1)} %get-tuple-element.68), channel_id=1, source_target_pairs={{0,8},{8,0},{16,24},{24,16},{1,9},{9,1},{17,25},{25,17},{2,10},{10... | collective-permute-start | bytes 786440 | tf_op jit(solution)/shard_map/ppermute | solution.py:36
  53.9 4.6 %collective-permute-done.12.r0.refs_2_ = bf16[4,128,256]{2,1,0:T(8,128)(2,1)S(1)} collective-permute-done((bf16[4,128,256]{2,1,0:T(8,128)(2,1)S(1)}, bf16[4,128,256]{2,1,0:T(8,128)(2,1)S(1)}, u32[]{:S(2)}, u32[]{:S(2)}) %collective-permute-start.12) | collective-permute-done | bytes 262176 | tf_op jit(solution)/shard_map/ppermute | solution.py:36
  58.5 3.5 %collective-permute-done.13.r1.refs_3_ = bf16[4,128,256]{2,1,0:T(8,128)(2,1)S(1)} collective-permute-done((bf16[4,128,256]{2,1,0:T(8,128)(2,1)S(1)}, bf16[4,128,256]{2,1,0:T(8,128)(2,1)S(1)}, u32[]{:S(2)}, u32[]{:S(2)}) %collective-permute-start.13) | collective-permute-done | bytes 262176 | tf_op jit(solution)/shard_map/ppermute | solution.py:36
  65.5 2.1 %collective-permute-done.14.refs_1_ = bf16[2,128,256]{2,1,0:T(8,128)(2,1)S(1)} collective-permute-done((bf16[2,128,256]{2,1,0:T(8,128)(2,1)S(1)}, bf16[2,128,256]{2,1,0:T(8,128)(2,1)S(1)}, u32[]{:S(2)}, u32[]{:S(2)}) %collective-permute-start.14) | collective-permute-done | bytes 131104 | tf_op jit(solution)/shard_map/ppermute | solution.py:36
  70.2 2.2 %collective-permute-start.19 = (bf16[4,128,256]{2,1,0:T(8,128)(2,1)S(1)}, bf16[4,128,256]{2,1,0:T(8,128)(2,1)S(1)}, u32[]{:S(2)}, u32[]{:S(2)}) collective-permute-start(bf16[4,128,256]{2,1,0:T(8,128)(2,1)S(1)} %get-tuple-element.80), channel_id=1, source_target_pairs={{0,24},{8,16},{16,8},{24,0},{1,25},{9,17},{17,9},{25,1},{2,26},{10... | collective-permute-start | bytes 786440 | tf_op jit(solution)/shard_map/ppermute | solution.py:36
  72.4 1.7 %collective-permute-start.22 = (bf16[4,128,256]{2,1,0:T(8,128)(2,1)S(1)}, bf16[4,128,256]{2,1,0:T(8,128)(2,1)S(1)}, u32[]{:S(2)}, u32[]{:S(2)}) collective-permute-start(bf16[4,128,256]{2,1,0:T(8,128)(2,1)S(1)} %get-tuple-element.85), channel_id=1, source_target_pairs={{0,2},{2,0},{4,6},{6,4},{1,3},{3,1},{5,7},{7,5},{8,10},{10,8},{12,... | collective-permute-start | bytes 786440 | tf_op jit(solution)/shard_map/ppermute | solution.py:36
  75.5 1.6 %collective-permute-done.18.r0.refs_2_ = bf16[4,128,256]{2,1,0:T(8,128)(2,1)S(1)} collective-permute-done((bf16[4,128,256]{2,1,0:T(8,128)(2,1)S(1)}, bf16[4,128,256]{2,1,0:T(8,128)(2,1)S(1)}, u32[]{:S(2)}, u32[]{:S(2)}) %collective-permute-start.18) | collective-permute-done | bytes 262176 | tf_op jit(solution)/shard_map/ppermute | solution.py:36
  77.1 5.0 %collective-permute-done.19.r1.refs_3_ = bf16[4,128,256]{2,1,0:T(8,128)(2,1)S(1)} collective-permute-done((bf16[4,128,256]{2,1,0:T(8,128)(2,1)S(1)}, bf16[4,128,256]{2,1,0:T(8,128)(2,1)S(1)}, u32[]{:S(2)}, u32[]{:S(2)}) %collective-permute-start.19) | collective-permute-done | bytes 262176 | tf_op jit(solution)/shard_map/ppermute | solution.py:36
  82.2 1.7 %collective-permute-start.20 = (bf16[2,128,256]{2,1,0:T(8,128)(2,1)S(1)}, bf16[2,128,256]{2,1,0:T(8,128)(2,1)S(1)}, u32[]{:S(2)}, u32[]{:S(2)}) collective-permute-start(bf16[2,128,256]{2,1,0:T(8,128)(2,1)S(1)} %get-tuple-element.81), channel_id=1, source_target_pairs={{0,2},{2,0},{4,6},{6,4},{1,3},{3,1},{5,7},{7,5},{8,10},{10,8},{12,... | collective-permute-start | bytes 393224 | tf_op jit(solution)/shard_map/ppermute | solution.py:36
  86.7 2.1 %shard_map.80 = (bf16[16,256,128]{2,1,0:T(8,128)(2,1)}, f32[4,4,256]{2,1,0:T(4,128)S(1)}, bf16[37,128,256]{2,1,0:T(8,128)(2,1)S(1)}) custom-call(s32[1,128]{1,0:T(1,128)S(1)} %pad_bitcast_fusion.refs_0_, bf16[16,128,256]{2,1,0:T(8,128)(2,1)S(1)} %get-tuple-element.84.refs_1_, bf16[4,128,256]{2,1,0:T(8,128)(2,1)S(1)} %collective-permute-done.18.r0.refs_2_, ...), custom_call_target="tpu_custom_call" | custom-call | flops 805306368 | bytes 1048576 | tf_op jit(solution)/shard_map/pallas_call | solution.py:45
  (51 shorter events, 27.3 us)
Async XLA Ops:
  2.3 9.8 %collective-permute-start = (bf16[4,128,256]{2,1,0:T(8,128)(2,1)S(1)}, bf16[4,128,256]{2,1,0:T(8,128)(2,1)S(1)}, u32[]{:S(2)}, u32[]{:S(2)}) collective-permute-start(bf16[4,128,256]{2,1,0:T(8,128)(2,1)S(1)} %get-tuple-element.47), channel_id=1, source_target_pairs={{0,8},{8,0},{16,24},{24,16},{1,9},{9,1},{17,25},{25,17},{2,10},{10... | collective-permute-start | bytes 786440 | tf_op jit(solution)/shard_map/ppermute | solution.py:36
  5.4 14.2 %collective-permute-start.1 = (bf16[4,128,256]{2,1,0:T(8,128)(2,1)S(1)}, bf16[4,128,256]{2,1,0:T(8,128)(2,1)S(1)}, u32[]{:S(2)}, u32[]{:S(2)}) collective-permute-start(bf16[4,128,256]{2,1,0:T(8,128)(2,1)S(1)} %get-tuple-element.48), channel_id=1, source_target_pairs={{0,24},{8,16},{16,8},{24,0},{1,25},{9,17},{17,9},{25,1},{2,26},{10... | collective-permute-start | bytes 786440 | tf_op jit(solution)/shard_map/ppermute | solution.py:36
  7.9 18.2 %collective-permute-start.4 = (bf16[4,128,256]{2,1,0:T(8,128)(2,1)S(1)}, bf16[4,128,256]{2,1,0:T(8,128)(2,1)S(1)}, u32[]{:S(2)}, u32[]{:S(2)}) collective-permute-start(bf16[4,128,256]{2,1,0:T(8,128)(2,1)S(1)} %get-tuple-element.52), channel_id=1, source_target_pairs={{0,2},{2,0},{4,6},{6,4},{1,3},{3,1},{5,7},{7,5},{8,10},{10,8},{12,... | collective-permute-start | bytes 786440 | tf_op jit(solution)/shard_map/ppermute | solution.py:36
  9.3 16.7 %collective-permute-start.5 = (bf16[4,128,256]{2,1,0:T(8,128)(2,1)S(1)}, bf16[4,128,256]{2,1,0:T(8,128)(2,1)S(1)}, u32[]{:S(2)}, u32[]{:S(2)}) collective-permute-start(bf16[4,128,256]{2,1,0:T(8,128)(2,1)S(1)} %get-tuple-element.53), channel_id=1, source_target_pairs={{0,6},{2,4},{4,2},{6,0},{1,7},{3,5},{5,3},{7,1},{8,14},{10,12},{12... | collective-permute-start | bytes 786440 | tf_op jit(solution)/shard_map/ppermute | solution.py:36
  19.6 7.7 %collective-permute-start.2 = (bf16[2,128,256]{2,1,0:T(8,128)(2,1)S(1)}, bf16[2,128,256]{2,1,0:T(8,128)(2,1)S(1)}, u32[]{:S(2)}, u32[]{:S(2)}) collective-permute-start(bf16[2,128,256]{2,1,0:T(8,128)(2,1)S(1)} %get-tuple-element.49), channel_id=1, source_target_pairs={{0,2},{2,0},{4,6},{6,4},{1,3},{3,1},{5,7},{7,5},{8,10},{10,8},{12,... | collective-permute-start | bytes 393224 | tf_op jit(solution)/shard_map/ppermute | solution.py:36
  21.2 6.6 %collective-permute-start.3 = (bf16[2,128,256]{2,1,0:T(8,128)(2,1)S(1)}, bf16[2,128,256]{2,1,0:T(8,128)(2,1)S(1)}, u32[]{:S(2)}, u32[]{:S(2)}) collective-permute-start(bf16[2,128,256]{2,1,0:T(8,128)(2,1)S(1)} %get-tuple-element.50), channel_id=1, source_target_pairs={{0,6},{2,4},{4,2},{6,0},{1,7},{3,5},{5,3},{7,1},{8,14},{10,12},{12... | collective-permute-start | bytes 393224 | tf_op jit(solution)/shard_map/ppermute | solution.py:36
  28.4 11.8 %collective-permute-start.6 = (bf16[4,128,256]{2,1,0:T(8,128)(2,1)S(1)}, bf16[4,128,256]{2,1,0:T(8,128)(2,1)S(1)}, u32[]{:S(2)}, u32[]{:S(2)}) collective-permute-start(bf16[4,128,256]{2,1,0:T(8,128)(2,1)S(1)} %get-tuple-element.57), channel_id=1, source_target_pairs={{0,8},{8,0},{16,24},{24,16},{1,9},{9,1},{17,25},{25,17},{2,10},{10... | collective-permute-start | bytes 786440 | tf_op jit(solution)/shard_map/ppermute | solution.py:36
  28.9 11.3 %collective-permute-start.7 = (bf16[4,128,256]{2,1,0:T(8,128)(2,1)S(1)}, bf16[4,128,256]{2,1,0:T(8,128)(2,1)S(1)}, u32[]{:S(2)}, u32[]{:S(2)}) collective-permute-start(bf16[4,128,256]{2,1,0:T(8,128)(2,1)S(1)} %get-tuple-element.58), channel_id=1, source_target_pairs={{0,24},{8,16},{16,8},{24,0},{1,25},{9,17},{17,9},{25,1},{2,26},{10... | collective-permute-start | bytes 786440 | tf_op jit(solution)/shard_map/ppermute | solution.py:36
  31.3 12.6 %collective-permute-start.10 = (bf16[4,128,256]{2,1,0:T(8,128)(2,1)S(1)}, bf16[4,128,256]{2,1,0:T(8,128)(2,1)S(1)}, u32[]{:S(2)}, u32[]{:S(2)}) collective-permute-start(bf16[4,128,256]{2,1,0:T(8,128)(2,1)S(1)} %get-tuple-element.63), channel_id=1, source_target_pairs={{0,2},{2,0},{4,6},{6,4},{1,3},{3,1},{5,7},{7,5},{8,10},{10,8},{12,... | collective-permute-start | bytes 786440 | tf_op jit(solution)/shard_map/ppermute | solution.py:36
  32.8 12.0 %collective-permute-start.11 = (bf16[4,128,256]{2,1,0:T(8,128)(2,1)S(1)}, bf16[4,128,256]{2,1,0:T(8,128)(2,1)S(1)}, u32[]{:S(2)}, u32[]{:S(2)}) collective-permute-start(bf16[4,128,256]{2,1,0:T(8,128)(2,1)S(1)} %get-tuple-element.64), channel_id=1, source_target_pairs={{0,6},{2,4},{4,2},{6,0},{1,7},{3,5},{5,3},{7,1},{8,14},{10,12},{12... | collective-permute-start | bytes 786440 | tf_op jit(solution)/shard_map/ppermute | solution.py:36
  40.3 5.7 %collective-permute-start.8 = (bf16[2,128,256]{2,1,0:T(8,128)(2,1)S(1)}, bf16[2,128,256]{2,1,0:T(8,128)(2,1)S(1)}, u32[]{:S(2)}, u32[]{:S(2)}) collective-permute-start(bf16[2,128,256]{2,1,0:T(8,128)(2,1)S(1)} %get-tuple-element.59), channel_id=1, source_target_pairs={{0,2},{2,0},{4,6},{6,4},{1,3},{3,1},{5,7},{7,5},{8,10},{10,8},{12,... | collective-permute-start | bytes 393224 | tf_op jit(solution)/shard_map/ppermute | solution.py:36
  41.8 6.3 %collective-permute-start.9 = (bf16[2,128,256]{2,1,0:T(8,128)(2,1)S(1)}, bf16[2,128,256]{2,1,0:T(8,128)(2,1)S(1)}, u32[]{:S(2)}, u32[]{:S(2)}) collective-permute-start(bf16[2,128,256]{2,1,0:T(8,128)(2,1)S(1)} %get-tuple-element.60), channel_id=1, source_target_pairs={{0,6},{2,4},{4,2},{6,0},{1,7},{3,5},{5,3},{7,1},{8,14},{10,12},{12... | collective-permute-start | bytes 393224 | tf_op jit(solution)/shard_map/ppermute | solution.py:36
  48.8 9.7 %collective-permute-start.12 = (bf16[4,128,256]{2,1,0:T(8,128)(2,1)S(1)}, bf16[4,128,256]{2,1,0:T(8,128)(2,1)S(1)}, u32[]{:S(2)}, u32[]{:S(2)}) collective-permute-start(bf16[4,128,256]{2,1,0:T(8,128)(2,1)S(1)} %get-tuple-element.68), channel_id=1, source_target_pairs={{0,8},{8,0},{16,24},{24,16},{1,9},{9,1},{17,25},{25,17},{2,10},{10... | collective-permute-start | bytes 786440 | tf_op jit(solution)/shard_map/ppermute | solution.py:36
  51.3 10.6 %collective-permute-start.13 = (bf16[4,128,256]{2,1,0:T(8,128)(2,1)S(1)}, bf16[4,128,256]{2,1,0:T(8,128)(2,1)S(1)}, u32[]{:S(2)}, u32[]{:S(2)}) collective-permute-start(bf16[4,128,256]{2,1,0:T(8,128)(2,1)S(1)} %get-tuple-element.69), channel_id=1, source_target_pairs={{0,24},{8,16},{16,8},{24,0},{1,25},{9,17},{17,9},{25,1},{2,26},{10... | collective-permute-start | bytes 786440 | tf_op jit(solution)/shard_map/ppermute | solution.py:36
  52.4 11.1 %collective-permute-start.16 = (bf16[4,128,256]{2,1,0:T(8,128)(2,1)S(1)}, bf16[4,128,256]{2,1,0:T(8,128)(2,1)S(1)}, u32[]{:S(2)}, u32[]{:S(2)}) collective-permute-start(bf16[4,128,256]{2,1,0:T(8,128)(2,1)S(1)} %get-tuple-element.74), channel_id=1, source_target_pairs={{0,2},{2,0},{4,6},{6,4},{1,3},{3,1},{5,7},{7,5},{8,10},{10,8},{12,... | collective-permute-start | bytes 786440 | tf_op jit(solution)/shard_map/ppermute | solution.py:36
  52.7 11.5 %collective-permute-start.17 = (bf16[4,128,256]{2,1,0:T(8,128)(2,1)S(1)}, bf16[4,128,256]{2,1,0:T(8,128)(2,1)S(1)}, u32[]{:S(2)}, u32[]{:S(2)}) collective-permute-start(bf16[4,128,256]{2,1,0:T(8,128)(2,1)S(1)} %get-tuple-element.75), channel_id=1, source_target_pairs={{0,6},{2,4},{4,2},{6,0},{1,7},{3,5},{5,3},{7,1},{8,14},{10,12},{12... | collective-permute-start | bytes 786440 | tf_op jit(solution)/shard_map/ppermute | solution.py:36
  62.0 5.6 %collective-permute-start.14 = (bf16[2,128,256]{2,1,0:T(8,128)(2,1)S(1)}, bf16[2,128,256]{2,1,0:T(8,128)(2,1)S(1)}, u32[]{:S(2)}, u32[]{:S(2)}) collective-permute-start(bf16[2,128,256]{2,1,0:T(8,128)(2,1)S(1)} %get-tuple-element.70), channel_id=1, source_target_pairs={{0,2},{2,0},{4,6},{6,4},{1,3},{3,1},{5,7},{7,5},{8,10},{10,8},{12,... | collective-permute-start | bytes 393224 | tf_op jit(solution)/shard_map/ppermute | solution.py:36
  62.4 5.9 %collective-permute-start.15 = (bf16[2,128,256]{2,1,0:T(8,128)(2,1)S(1)}, bf16[2,128,256]{2,1,0:T(8,128)(2,1)S(1)}, u32[]{:S(2)}, u32[]{:S(2)}) collective-permute-start(bf16[2,128,256]{2,1,0:T(8,128)(2,1)S(1)} %get-tuple-element.71), channel_id=1, source_target_pairs={{0,6},{2,4},{4,2},{6,0},{1,7},{3,5},{5,3},{7,1},{8,14},{10,12},{12... | collective-permute-start | bytes 393224 | tf_op jit(solution)/shard_map/ppermute | solution.py:36
  68.9 8.2 %collective-permute-start.18 = (bf16[4,128,256]{2,1,0:T(8,128)(2,1)S(1)}, bf16[4,128,256]{2,1,0:T(8,128)(2,1)S(1)}, u32[]{:S(2)}, u32[]{:S(2)}) collective-permute-start(bf16[4,128,256]{2,1,0:T(8,128)(2,1)S(1)} %get-tuple-element.79), channel_id=1, source_target_pairs={{0,8},{8,0},{16,24},{24,16},{1,9},{9,1},{17,25},{25,17},{2,10},{10... | collective-permute-start | bytes 786440 | tf_op jit(solution)/shard_map/ppermute | solution.py:36
  70.2 11.9 %collective-permute-start.19 = (bf16[4,128,256]{2,1,0:T(8,128)(2,1)S(1)}, bf16[4,128,256]{2,1,0:T(8,128)(2,1)S(1)}, u32[]{:S(2)}, u32[]{:S(2)}) collective-permute-start(bf16[4,128,256]{2,1,0:T(8,128)(2,1)S(1)} %get-tuple-element.80), channel_id=1, source_target_pairs={{0,24},{8,16},{16,8},{24,0},{1,25},{9,17},{17,9},{25,1},{2,26},{10... | collective-permute-start | bytes 786440 | tf_op jit(solution)/shard_map/ppermute | solution.py:36
  72.4 13.0 %collective-permute-start.22 = (bf16[4,128,256]{2,1,0:T(8,128)(2,1)S(1)}, bf16[4,128,256]{2,1,0:T(8,128)(2,1)S(1)}, u32[]{:S(2)}, u32[]{:S(2)}) collective-permute-start(bf16[4,128,256]{2,1,0:T(8,128)(2,1)S(1)} %get-tuple-element.85), channel_id=1, source_target_pairs={{0,2},{2,0},{4,6},{6,4},{1,3},{3,1},{5,7},{7,5},{8,10},{10,8},{12,... | collective-permute-start | bytes 786440 | tf_op jit(solution)/shard_map/ppermute | solution.py:36
  74.1 12.6 %collective-permute-start.23 = (bf16[4,128,256]{2,1,0:T(8,128)(2,1)S(1)}, bf16[4,128,256]{2,1,0:T(8,128)(2,1)S(1)}, u32[]{:S(2)}, u32[]{:S(2)}) collective-permute-start(bf16[4,128,256]{2,1,0:T(8,128)(2,1)S(1)} %get-tuple-element.86), channel_id=1, source_target_pairs={{0,6},{2,4},{4,2},{6,0},{1,7},{3,5},{5,3},{7,1},{8,14},{10,12},{12... | collective-permute-start | bytes 786440 | tf_op jit(solution)/shard_map/ppermute | solution.py:36
  82.2 6.7 %collective-permute-start.20 = (bf16[2,128,256]{2,1,0:T(8,128)(2,1)S(1)}, bf16[2,128,256]{2,1,0:T(8,128)(2,1)S(1)}, u32[]{:S(2)}, u32[]{:S(2)}) collective-permute-start(bf16[2,128,256]{2,1,0:T(8,128)(2,1)S(1)} %get-tuple-element.81), channel_id=1, source_target_pairs={{0,2},{2,0},{4,6},{6,4},{1,3},{3,1},{5,7},{7,5},{8,10},{10,8},{12,... | collective-permute-start | bytes 393224 | tf_op jit(solution)/shard_map/ppermute | solution.py:36
  83.9 6.4 %collective-permute-start.21 = (bf16[2,128,256]{2,1,0:T(8,128)(2,1)S(1)}, bf16[2,128,256]{2,1,0:T(8,128)(2,1)S(1)}, u32[]{:S(2)}, u32[]{:S(2)}) collective-permute-start(bf16[2,128,256]{2,1,0:T(8,128)(2,1)S(1)} %get-tuple-element.82), channel_id=1, source_target_pairs={{0,6},{2,4},{4,2},{6,0},{1,7},{3,5},{5,3},{7,1},{8,14},{10,12},{12... | collective-permute-start | bytes 393224 | tf_op jit(solution)/shard_map/ppermute | solution.py:36
  (3 other events, 19.4 us)
